TPU v7x, 32 devices: a whole 2x2x4 slice. The times are simulated.
32 devices in a mesh: dp: 4 (over y, x), spatial: 8 (over z, core).
Axes of the slice: x: 2, y: 2, z: 4, core: 2. Of those that a mesh axis runs over, the one named last changes fastest.
Arguments:
- volume: bfloat16 [4, 16, 16, 8, 128], P('dp', 'spatial'), may hold values from -6 to 6
- cotangent: bfloat16 [4, 16, 16, 8, 128], P('dp', 'spatial'), may hold values from -6 to 6
- master: float32 [3456, 128], P('dp'), may hold values from -0.109375 to 0.109375
- moment: float32 [3456, 128], P('dp'), may hold values from -6 to 6
- second: float32 [3456, 128], P('dp'), may hold values from 0.25 to 4
Outputs:
- activation: bfloat16 [4, 16, 16, 8, 128], P('dp', 'spatial')
- input_grad: bfloat16 [4, 16, 16, 8, 128], P('dp', 'spatial')
- master_next: float32 [3456, 128], P('dp')
- moment_next: float32 [3456, 128], P('dp')
- second_next: float32 [3456, 128], P('dp')
All inputs are finite; a program needn't handle non-finite values.
Results may differ from a plain program's by a relative error of at most 0.002.
The roundings to bfloat16 on the way count: a program that leaves them out, or rounds other values in their place, can miss the bound.
Values may be sent and summed in bfloat16 or wider, within the bound.
A program may use at most 64 MiB of HBM per device.

v0:
```python
import math

import jax
import jax.numpy as jnp
from jax import lax
from jax.sharding import PartitionSpec as P


def with_halo(block, sides, width):
    for axis, dim in sides:
        count = lax.axis_size(axis)
        forward = [(i, i + 1) for i in range(count - 1)]
        backward = [(target, source) for source, target in forward]
        low = lax.ppermute(
            lax.slice_in_dim(block, block.shape[dim] - width, None, axis=dim), axis, forward
        )
        high = lax.ppermute(lax.slice_in_dim(block, 0, width, axis=dim), axis, backward)
        block = jnp.concatenate([low, block, high], axis=dim)
    return block


def silu_slope(preact):
    sigma = jax.nn.sigmoid(preact)
    return sigma * (1.0 + preact * (1.0 - sigma))


def pad_sides(field):
    return jnp.pad(field, ((0, 0), (1, 1), (1, 1), (0, 0)))


def forward_taps(padded, kernel, planes, rows, cols):
    width = kernel.shape[1]
    total = jnp.zeros((planes * rows * cols, width), jnp.float32)
    for offset_z in range(3):
        for offset_y in range(3):
            for offset_x in range(3):
                tap_index = offset_z * 9 + offset_y * 3 + offset_x
                piece = padded[
                    offset_z : offset_z + planes,
                    offset_y : offset_y + rows,
                    offset_x : offset_x + cols,
                ].reshape(-1, width)
                total = total + jnp.dot(
                    piece, kernel[tap_index], preferred_element_type=jnp.float32
                )
    return total


def backward_taps(grad_pad, kernel, planes, rows, cols):
    width = kernel.shape[1]
    total = jnp.zeros((planes * rows * cols, width), jnp.float32)
    for offset_z in range(3):
        for offset_y in range(3):
            for offset_x in range(3):
                tap_index = offset_z * 9 + offset_y * 3 + offset_x
                piece = grad_pad[
                    2 - offset_z : 2 - offset_z + planes,
                    2 - offset_y : 2 - offset_y + rows,
                    2 - offset_x : 2 - offset_x + cols,
                ].reshape(-1, width)
                total = total + lax.dot_general(
                    piece,
                    kernel[tap_index],
                    (((1,), (1,)), ((), ())),
                    preferred_element_type=jnp.float32,
                )
    return total


def weight_taps(padded, hidden_grad, planes, rows, cols):
    width = hidden_grad.shape[1]
    blocks = []
    for offset_z in range(3):
        for offset_y in range(3):
            for offset_x in range(3):
                piece = padded[
                    offset_z : offset_z + planes,
                    offset_y : offset_y + rows,
                    offset_x : offset_x + cols,
                ].reshape(-1, width)
                blocks.append(
                    lax.dot_general(
                        piece,
                        hidden_grad,
                        (((0,), (0,)), ((), ())),
                        preferred_element_type=jnp.float32,
                    )
                )
    return jnp.concatenate(blocks, axis=0)


def per_device(volume, cotangent, master, moment, second):
    planes = volume.shape[1]
    rows = volume.shape[2]
    cols = volume.shape[3]
    width = volume.shape[4]
    kernel = lax.all_gather(master.astype(jnp.bfloat16), "dp", axis=0, tiled=True).reshape(
        27, width, width
    )
    wide = with_halo(volume, (("spatial", 1),), 1)[0]
    padded = pad_sides(wide)
    preact = forward_taps(padded, kernel, planes, rows, cols)
    activated = jax.nn.silu(preact).astype(jnp.bfloat16)
    hidden_grad = (cotangent[0].reshape(-1, width).astype(jnp.float32) * silu_slope(preact)).astype(
        jnp.bfloat16
    )
    grad_block = hidden_grad.reshape(1, planes, rows, cols, width)
    wide_grad = with_halo(grad_block, (("spatial", 1),), 1)[0]
    grad_pad = pad_sides(wide_grad)
    input_grad = backward_taps(grad_pad, kernel, planes, rows, cols).astype(jnp.bfloat16)
    local_grad = weight_taps(padded, hidden_grad, planes, rows, cols)
    partial_grad = lax.psum_scatter(
        local_grad.astype(jnp.bfloat16), "dp", scatter_dimension=0, tiled=True
    ).astype(jnp.float32)
    shard = lax.psum(partial_grad, "spatial")
    cells_all = lax.axis_size("dp") * lax.axis_size("spatial") * planes * rows * cols
    weight_grad = shard / math.sqrt(cells_all)
    moment_next = 0.9 * moment + 0.1 * weight_grad
    second_next = 0.999 * second + 0.001 * weight_grad * weight_grad
    master_next = master - 0.001 * (moment_next / (jnp.sqrt(second_next) + 1e-08) + 0.01 * master)
    activation = activated.reshape(1, planes, rows, cols, width)
    input_block = input_grad.reshape(1, planes, rows, cols, width)
    return (activation, input_block, master_next, moment_next, second_next)


def solution(mesh):
    return jax.shard_map(
        per_device,
        mesh=mesh,
        in_specs=(
            P("dp", "spatial", None, None, None),
            P("dp", "spatial", None, None, None),
            P("dp", None),
            P("dp", None),
            P("dp", None),
        ),
        out_specs=(
            P("dp", "spatial", None, None, None),
            P("dp", "spatial", None, None, None),
            P("dp", None),
            P("dp", None),
            P("dp", None),
        ),
        check_vma=False,
    )
```

profile of v0, /device:TPU:0, one launch (start us, length us, event | category | flops | bytes accessed | tf_op | source)
XLA Modules:
  0.0 116.7 jit_solution(8562241958036103037)
XLA Ops:
  7.2 0.8 fusion.95
  8.0 2.4 %collective-permute-start = (bf16[1,1,16,8,128]{4,3,2,1,0:T(8,128)(2,1)S(1)}, bf16[1,1,16,8,128]{4,3,2,1,0:T(8,128)(2,1)S(1)}, u32[]{:S(2)}, u32[]{:S(2)}) collective-permute-start(bf16[1,1,16,8,128]{4,3,2,1,0:T(8,128)(2,1)S(1)} %get-tuple-element.64), channel_id=1, source_target_pairs={{0,1},{1,2},{2,3},{3,4},{4,5},{5,6},{6,7},{8,9},{9,10},{10,11},{11... | collective-permute-start | bytes 98312 | tf_op jit(solution)/shard_map/ppermute | solution.py:14
  10.4 1.3 %collective-permute-start.1 = (bf16[1,1,16,8,128]{4,3,2,1,0:T(8,128)(2,1)S(1)}, bf16[1,1,16,8,128]{4,3,2,1,0:T(8,128)(2,1)S(1)}, u32[]{:S(2)}, u32[]{:S(2)}) collective-permute-start(bf16[1,1,16,8,128]{4,3,2,1,0:T(8,128)(2,1)S(1)} %get-tuple-element.65), channel_id=1, source_target_pairs={{1,0},{2,1},{3,2},{4,3},{5,4},{6,5},{7,6},{9,8},{10,9},{11,10},{12... | collective-permute-start | bytes 98312 | tf_op jit(solution)/shard_map/ppermute | solution.py:17
  11.7 1.0 convert_element_type.25
  12.7 14.2 %all_gather.3 = bf16[3456,128]{1,0:T(8,128)(2,1)S(1)} all-gather(bf16[864,128]{1,0:T(8,128)(2,1)S(1)} %convert_element_type.25), channel_id=1, replica_groups=mesh['dp'=4,'spatial'=8] {'dp'}, dimensions={0}, use_global_device_ids=true | all-gather | bytes 1105920 | tf_op jit(solution)/shard_map/all_gather | solution.py:97
  27.0 0.2 pad_slice_fusion.24
  31.2 0.7 copy-done.5
  31.9 0.8 fusion.33
  32.9 0.2 fusion.29
  33.1 0.2 fusion.28
  33.4 0.2 fusion.27
  33.6 0.2 fusion.26
  33.8 0.2 fusion.25
  34.2 0.2 fusion.23
  34.6 0.2 fusion.21
  34.8 0.2 fusion.20
  35.0 0.2 fusion.19
  35.4 0.2 fusion.32
  36.1 0.2 fusion.15
  36.5 0.2 fusion.13
  36.7 0.2 fusion.12
  36.9 0.2 fusion.11
  37.3 0.2 fusion.9
  37.8 0.2 fusion.7
  38.2 2.4 %collective-permute-start.2 = (bf16[1,1,16,8,128]{4,3,2,1,0:T(8,128)(2,1)S(1)}, bf16[1,1,16,8,128]{4,3,2,1,0:T(8,128)(2,1)S(1)}, u32[]{:S(2)}, u32[]{:S(2)}) collective-permute-start(bf16[1,1,16,8,128]{4,3,2,1,0:T(8,128)(2,1)S(1)} %get-tuple-element.60), channel_id=1, source_target_pairs={{0,1},{1,2},{2,3},{3,4},{4,5},{5,6},{6,7},{8,9},{9,10},{10,11},{11... | collective-permute-start | bytes 98312 | tf_op jit(solution)/shard_map/ppermute | solution.py:14
  40.6 1.3 %collective-permute-start.3 = (bf16[1,1,16,8,128]{4,3,2,1,0:T(8,128)(2,1)S(1)}, bf16[1,1,16,8,128]{4,3,2,1,0:T(8,128)(2,1)S(1)}, u32[]{:S(2)}, u32[]{:S(2)}) collective-permute-start(bf16[1,1,16,8,128]{4,3,2,1,0:T(8,128)(2,1)S(1)} %get-tuple-element.61), channel_id=1, source_target_pairs={{1,0},{2,1},{3,2},{4,3},{5,4},{6,5},{7,6},{9,8},{10,9},{11,10},{12... | collective-permute-start | bytes 98312 | tf_op jit(solution)/shard_map/ppermute | solution.py:17
  42.1 0.9 copy-done.2
  43.0 3.1 %collective-permute-done.3 = bf16[1,1,16,8,128]{4,3,2,1,0:T(8,128)(2,1)S(1)} collective-permute-done((bf16[1,1,16,8,128]{4,3,2,1,0:T(8,128)(2,1)S(1)}, bf16[1,1,16,8,128]{4,3,2,1,0:T(8,128)(2,1)S(1)}, u32[]{:S(2)}, u32[]{:S(2)}) %collective-permute-start.3) | collective-permute-done | bytes 32800 | tf_op jit(solution)/shard_map/ppermute | solution.py:17
  50.9 0.8 fusion.4
  51.7 22.4 %reduce-scatter.2.cloned.1.call-done = bf16[864,128]{1,0:T(8,128)(2,1)} async-done(((bf16[3456,128]{1,0:T(8,128)(2,1)}), bf16[864,128]{1,0:T(8,128)(2,1)}) %reduce-scatter.2.cloned.1.call-update) | async-done | bytes 221200 | tf_op jit(solution)/shard_map/reduce_scatter | solution.py:112
  74.1 34.5 %all-reduce.3 = f32[864,128]{1,0:T(8,128)S(1)} all-reduce(bf16[864,128]{1,0:T(8,128)(2,1)} %reduce-scatter.2.cloned.1.call-done), channel_id=1, replica_groups=mesh['dp'=4,'spatial'=8] {'spatial'}, use_global_device_ids=true, to_apply=%region_1.2 | all-reduce | flops 110592 | bytes 663552 | tf_op jit(solution)/shard_map/psum | solution.py:115
  108.7 1.2 %multiply_subtract_fusion = (f32[864,128]{1,0:T(8,128)}, f32[864,128]{1,0:T(8,128)}, f32[864,128]{1,0:T(8,128)}) fusion(f32[864,128]{1,0:T(8,128)S(1)} %copy-done, f32[864,128]{1,0:T(8,128)S(1)} %all-reduce.3, f32[864,128]{1,0:T(8,128)S(1)} %copy-done.3, f32[864,128]{1,0:T(8,128)S(1)} %copy-done.4), kind=kLoop, calls=%fused_computation.156 | loop fusion | flops 1548288 | bytes 3096576 | tf_op jit(solution)/shard_map/sub | solution.py:120
  (86 shorter events, 10.8 us)
Async XLA Ops:
  7.2 66.9 %reduce-scatter.2.cloned.1.call-start = ((), (), s32[]{:S(2)}) async-start(), calls=%async_computation.1 | async-start | bytes 1105920 | tf_op jit(solution)/shard_map/reduce_scatter | solution.py:112
  8.0 18.9 %collective-permute-start = (bf16[1,1,16,8,128]{4,3,2,1,0:T(8,128)(2,1)S(1)}, bf16[1,1,16,8,128]{4,3,2,1,0:T(8,128)(2,1)S(1)}, u32[]{:S(2)}, u32[]{:S(2)}) collective-permute-start(bf16[1,1,16,8,128]{4,3,2,1,0:T(8,128)(2,1)S(1)} %get-tuple-element.64), channel_id=1, source_target_pairs={{0,1},{1,2},{2,3},{3,4},{4,5},{5,6},{6,7},{8,9},{9,10},{10,11},{11... | collective-permute-start | bytes 98312 | tf_op jit(solution)/shard_map/ppermute | solution.py:14
  10.4 16.5 %collective-permute-start.1 = (bf16[1,1,16,8,128]{4,3,2,1,0:T(8,128)(2,1)S(1)}, bf16[1,1,16,8,128]{4,3,2,1,0:T(8,128)(2,1)S(1)}, u32[]{:S(2)}, u32[]{:S(2)}) collective-permute-start(bf16[1,1,16,8,128]{4,3,2,1,0:T(8,128)(2,1)S(1)} %get-tuple-element.65), channel_id=1, source_target_pairs={{1,0},{2,1},{3,2},{4,3},{5,4},{6,5},{7,6},{9,8},{10,9},{11,10},{12... | collective-permute-start | bytes 98312 | tf_op jit(solution)/shard_map/ppermute | solution.py:17
  12.7 14.2 %copy-start.1 = (bf16[1,2,16,8,128]{4,3,2,1,0:T(8,128)(2,1)S(1)}, bf16[1,2,16,8,128]{4,3,2,1,0:T(8,128)(2,1)}, u32[]{:S(2)}) copy-start(bf16[1,2,16,8,128]{4,3,2,1,0:T(8,128)(2,1)} %param.5) | copy-start | bytes 196612
  31.1 0.8 copy-start.5
  38.2 4.8 %collective-permute-start.2 = (bf16[1,1,16,8,128]{4,3,2,1,0:T(8,128)(2,1)S(1)}, bf16[1,1,16,8,128]{4,3,2,1,0:T(8,128)(2,1)S(1)}, u32[]{:S(2)}, u32[]{:S(2)}) collective-permute-start(bf16[1,1,16,8,128]{4,3,2,1,0:T(8,128)(2,1)S(1)} %get-tuple-element.60), channel_id=1, source_target_pairs={{0,1},{1,2},{2,3},{3,4},{4,5},{5,6},{6,7},{8,9},{9,10},{10,11},{11... | collective-permute-start | bytes 98312 | tf_op jit(solution)/shard_map/ppermute | solution.py:14
  40.6 5.6 %collective-permute-start.3 = (bf16[1,1,16,8,128]{4,3,2,1,0:T(8,128)(2,1)S(1)}, bf16[1,1,16,8,128]{4,3,2,1,0:T(8,128)(2,1)S(1)}, u32[]{:S(2)}, u32[]{:S(2)}) collective-permute-start(bf16[1,1,16,8,128]{4,3,2,1,0:T(8,128)(2,1)S(1)} %get-tuple-element.61), channel_id=1, source_target_pairs={{1,0},{2,1},{3,2},{4,3},{5,4},{6,5},{7,6},{9,8},{10,9},{11,10},{12... | collective-permute-start | bytes 98312 | tf_op jit(solution)/shard_map/ppermute | solution.py:17
  42.1 0.9 copy-start.2
  50.5 58.1 %copy-start.4 = (f32[864,128]{1,0:T(8,128)S(1)}, f32[864,128]{1,0:T(8,128)}, u32[]{:S(2)}) copy-start(f32[864,128]{1,0:T(8,128)} %param.8) | copy-start | bytes 1327108
  50.9 57.8 %copy-start = (f32[864,128]{1,0:T(8,128)S(1)}, f32[864,128]{1,0:T(8,128)}, u32[]{:S(2)}) copy-start(f32[864,128]{1,0:T(8,128)} %param.7) | copy-start | bytes 1327108
  50.9 57.8 %copy-start.3 = (f32[864,128]{1,0:T(8,128)S(1)}, f32[864,128]{1,0:T(8,128)}, u32[]{:S(2)}) copy-start(f32[864,128]{1,0:T(8,128)} %param.9) | copy-start | bytes 1327108
Sparse Core Ops, SparseCore 0:
  43.1 30.9 reduce-scatter.1
where the time goes:
time: 117 us
  blocking collectives  48.7 us (42%)
  waiting for transfers between devices  25.6 us (22%)
  matrix products  15.3 us (13%)
  between operations  14.6 us (12%)
  starting transfers between devices  7.38 us (6%)
  local copies, waits for them, and re-layouts  2.93 us (3%)
  other arithmetic  2.34 us (2%)
    psum x1, blocking collectives, per_device(): shard = lax.psum(partial_grad, 'spatial')  34.5 us
    reduce_scatter x1, waiting for transfers between devices, per_device(): lax.psum_scatter(local_grad.astype(jnp.bfloat16), 'dp', scatter_dimension...  22.4 us
    all_gather x1, blocking collectives, per_device(): lax.all_gather(master.astype(jnp.bfloat16), 'dp', axis=0, tiled=True)  14.2 us
    dot_general x27, matrix products, weight_taps(): lax.dot_general(piece, hidden_grad, (((0,), (0,)), ((), ())), preferred_e...  5.53 us
    dot_general x27, matrix products, backward_taps(): lax.dot_general(piece, kernel[tap_index], (((1,), (1,)), ((), ())), prefe...  5.07 us
    ppermute x2, starting transfers between devices, with_halo(): lax.ppermute(lax.slice_in_dim(block, block.shape[dim] - width, None, axis...  4.76 us
    dot_general x27, matrix products, forward_taps(): jnp.dot(piece, kernel[tap_index], preferred_element_type=jnp.float32)  4.67 us
    ppermute x2, waiting for transfers between devices, with_halo(): lax.ppermute(lax.slice_in_dim(block, 0, width, axis=dim), axis, backward)  3.13 us
  transfers between devices with their start and end apart: 5, of which 2 were waited for; matrix products, arithmetic and copies ran while one was open for 6% of the time, Pallas kernels for 0%

commit v1 on v0

v1 whole, which is shorter than its diff:
```python
import functools
import math

import jax
import jax.numpy as jnp
from jax import lax
from jax.experimental import pallas as pl
from jax.experimental.pallas import tpu as pltpu
from jax.sharding import PartitionSpec as P

MESH = pl.DeviceIdType.MESH
TILE = 16
CORES = 2


def shifted(plane, cols, step_y, step_x):
    area, width = plane.shape
    column = lax.broadcasted_iota(jnp.int32, (area, width), 0) % cols
    if step_x < 0:
        plane = jnp.where(column == 0, 0.0, pltpu.roll(plane, 1, 0))
    elif step_x > 0:
        plane = jnp.where(column == cols - 1, 0.0, pltpu.roll(plane, area - 1, 0))
    edge = jnp.zeros((cols, width), jnp.float32)
    if step_y < 0:
        plane = jnp.concatenate([edge, plane[: area - cols]], axis=0)
    elif step_y > 0:
        plane = jnp.concatenate([plane[cols:], edge], axis=0)
    return plane


def layer_kernel(
    sizes,
    volume,
    cotangent,
    master,
    moment,
    second,
    activation,
    input_grad,
    master_next,
    moment_next,
    second_next,
    kernel,
    halo,
    grad_halo,
    hidden,
    columns,
    turned,
    local_grad,
    local_sent,
    pair_got,
    chip_sent,
    chip_got,
    own_sum,
    slab_sent,
    slab_got,
    total,
    halo_s,
    halo_r,
    gh_s,
    gh_r,
    ag_s,
    ag_r,
    fw_s,
    fw_r,
    pr_s,
    pr_r,
    ch_s,
    ch_r,
    sl_s,
    sl_r,
    to_s,
    to_r,
    tf_s,
    tf_r,
):
    dps, slabs, planes, area, cols, cells_all = sizes
    chips = slabs // CORES
    width = volume.shape[1]
    rows = master.shape[0]
    half = rows // CORES
    piece = total.shape[2]
    dp = lax.axis_index("dp")
    slab = lax.axis_index("spatial")
    core = slab % CORES
    chip = slab // CORES
    other = 1 - core
    pair = chip * CORES + other
    block = planes * area

    def copy(src, dst, send, recv, target):
        return pltpu.make_async_remote_copy(
            src_ref=src,
            dst_ref=dst,
            send_sem=send,
            recv_sem=recv,
            device_id=target,
            device_id_type=MESH,
        )

    barrier = pltpu.get_barrier_semaphore()
    for step in range(1, dps):
        pl.semaphore_signal(
            barrier, inc=1, device_id=((dp + step) % dps, slab), device_id_type=MESH
        )
    for step in range(1, slabs):
        pl.semaphore_signal(
            barrier, inc=1, device_id=(dp, (slab + step) % slabs), device_id_type=MESH
        )

    def kernel_half(shard, which):
        return kernel.at[pl.ds(pl.multiple_of(shard * rows + which * half, TILE), half)]

    kernel[pl.ds(pl.multiple_of(dp * rows, TILE), rows)] = master[...].astype(jnp.bfloat16)
    pl.semaphore_wait(barrier, dps - 1 + slabs - 1)

    def halo_copy(source, dest, send, recv, side):
        if side == 0:
            return copy(
                source.at[pl.ds(block - area, area)], dest.at[0], send.at[0], recv.at[0], (dp, slab + 1)
            )
        return copy(source.at[pl.ds(0, area)], dest.at[1], send.at[1], recv.at[1], (dp, slab - 1))

    def halo_start(source, dest, send, recv):
        @pl.when(slab < slabs - 1)
        def _():
            halo_copy(source, dest, send, recv, 0).start()

        @pl.when(slab > 0)
        def _():
            halo_copy(source, dest, send, recv, 1).start()

    def halo_sent(source, dest, send, recv):
        @pl.when(slab < slabs - 1)
        def _():
            halo_copy(source, dest, send, recv, 0).wait_send()

        @pl.when(slab > 0)
        def _():
            halo_copy(source, dest, send, recv, 1).wait_send()

    def halo_wait(source, dest, send, recv):
        @pl.when(slab > 0)
        def _():
            halo_copy(source, dest, send, recv, 0).wait_recv()

        @pl.when(slab < slabs - 1)
        def _():
            halo_copy(source, dest, send, recv, 1).wait_recv()

        @pl.when(slab == 0)
        def _():
            dest[0] = jnp.zeros((area, width), jnp.bfloat16)

        @pl.when(slab == slabs - 1)
        def _():
            dest[1] = jnp.zeros((area, width), jnp.bfloat16)

    def gather_copy(shard, target):
        mine = kernel_half(shard, core)
        return copy(mine, mine, ag_s.at[target], ag_r.at[shard], (target, slab))

    def relay_copy(shard, which):
        mine = kernel_half(shard, which)
        return copy(mine, mine, fw_s.at[shard], fw_r.at[shard], (dp, pair))

    for step in range(1, dps):
        gather_copy(dp, (dp + step) % dps).start()
    halo_start(volume, halo, halo_s, halo_r)

    def put_columns(plane, at, sign, turn):
        plane = plane.astype(jnp.float32)
        for e in range(3):
            for f in range(3):
                moved = shifted(plane, cols, sign * (e - 1), sign * (f - 1)).astype(jnp.bfloat16)
                tap = e * 3 + f
                columns[at * area : (at + 1) * area, tap * width : (tap + 1) * width] = moved
                if turn:
                    turned[tap * width : (tap + 1) * width, at * area : (at + 1) * area] = moved.T

    for plane in range(planes):
        put_columns(volume[plane * area : (plane + 1) * area], plane + 1, 1, True)
    halo_wait(volume, halo, halo_s, halo_r)
    put_columns(halo[0], 0, 1, True)
    put_columns(halo[1], planes + 1, 1, True)

    for step in range(1, dps):
        source = (dp + step) % dps
        gather_copy(source, dp).wait_recv()
        relay_copy(source, core).start()
    for step in range(1, dps):
        relay_copy((dp + step) % dps, other).wait_recv()

    group = 9 * width
    preact = jnp.zeros((block, width), jnp.float32)
    for a in range(3):
        preact = preact + jnp.dot(
            columns[a * area : a * area + block, :],
            kernel[a * group : (a + 1) * group, :],
            preferred_element_type=jnp.float32,
        )
    sigma = jax.nn.sigmoid(preact)
    activation[...] = (preact * sigma).astype(jnp.bfloat16)
    slope = sigma * (1.0 + preact * (1.0 - sigma))
    hidden[...] = (cotangent[...].astype(jnp.float32) * slope).astype(jnp.bfloat16)

    def pair_copy(shard, which):
        at = pl.ds(pl.multiple_of(shard * rows + which * half, TILE), half)
        return copy(
            local_sent.at[at], pair_got.at[shard], pr_s.at[shard], pr_r.at[shard], (dp, pair)
        )

    next_shard = 0
    for a in range(3):
        part = jnp.dot(
            turned[:, a * area : a * area + block],
            hidden[...],
            preferred_element_type=jnp.float32,
        )
        local_grad[a * group : (a + 1) * group, :] = part
        local_sent[a * group : (a + 1) * group, :] = part.astype(jnp.bfloat16)
        while next_shard < dps and (next_shard + 1) * rows <= (a + 1) * group:
            pair_copy(next_shard, other).start()
            next_shard += 1
        if a == 0:
            halo_start(hidden, grad_halo, gh_s, gh_r)

    def own_rows(shard):
        return local_grad[pl.ds(pl.multiple_of(shard * rows + core * half, TILE), half), :]

    def chip_copy(shard, source):
        return copy(
            chip_sent.at[shard], chip_got.at[source], ch_s.at[shard], ch_r.at[source], (shard, slab)
        )

    for step in range(1, dps):
        shard = (dp + step) % dps
        pair_copy(shard, core).wait_recv()
        chip_sent[shard] = (own_rows(shard) + pair_got[shard].astype(jnp.float32)).astype(
            jnp.bfloat16
        )
        chip_copy(shard, dp).start()
    pair_copy(dp, core).wait_recv()
    own_sum[...] = own_rows(dp) + pair_got[dp].astype(jnp.float32)

    halo_wait(hidden, grad_halo, gh_s, gh_r)
    for plane in range(planes):
        put_columns(hidden[plane * area : (plane + 1) * area], plane + 1, -1, False)
    put_columns(grad_halo[0], 0, -1, False)
    put_columns(grad_halo[1], planes + 1, -1, False)
    back = jnp.zeros((block, width), jnp.float32)
    for a in range(3):
        for tap in range(9):
            at = (a * 9 + tap) * width
            back = back + lax.dot_general(
                columns[(2 - a) * area : (2 - a) * area + block, tap * width : (tap + 1) * width],
                kernel[at : at + width, :],
                (((1,), (1,)), ((), ())),
                preferred_element_type=jnp.float32,
            )
    input_grad[...] = back.astype(jnp.bfloat16)

    for step in range(1, dps):
        source = (dp + step) % dps
        chip_copy(dp, source).wait_recv()
        own_sum[...] += chip_got[source].astype(jnp.float32)
    slab_sent[...] = own_sum[...].astype(jnp.bfloat16)

    def start_of(index):
        return jnp.minimum(index * piece, half - piece)

    def slab_copy(owner, source):
        at = pl.ds(pl.multiple_of(start_of(owner), TILE), piece)
        return copy(
            slab_sent.at[at],
            slab_got.at[source],
            sl_s.at[owner],
            sl_r.at[source],
            (dp, owner * CORES + core),
        )

    for step in range(1, chips):
        slab_copy((chip + step) % chips, chip).start()
    piece_sum = own_sum[pl.ds(pl.multiple_of(start_of(chip), TILE), piece), :]
    for step in range(1, chips):
        source = (chip + step) % chips
        slab_copy(chip, source).wait_recv()
        piece_sum = piece_sum + slab_got[source].astype(jnp.float32)
    total[core, chip] = piece_sum.astype(jnp.bfloat16)

    def total_copy(source, target):
        ref = total.at[core, source]
        return copy(ref, ref, to_s.at[target], to_r.at[source], (dp, target * CORES + core))

    def total_relay(source, which):
        ref = total.at[which, source]
        return copy(ref, ref, tf_s.at[source], tf_r.at[source], (dp, pair))

    for step in range(1, chips):
        total_copy(chip, (chip + step) % chips).start()
    total_relay(chip, core).start()
    for step in range(1, chips):
        source = (chip + step) % chips
        total_copy(source, chip).wait_recv()
        total_relay(source, core).start()
    for step in range(chips):
        total_relay((chip + step) % chips, other).wait_recv()

    scale = 1.0 / math.sqrt(cells_all)
    for which in range(CORES):
        for index in range(chips):
            at = which * half + min(index * piece, half - piece)
            end = at + piece
            grad = total[which, index].astype(jnp.float32) * scale
            old = master[at:end, :]
            first = 0.9 * moment[at:end, :] + 0.1 * grad
            square = 0.999 * second[at:end, :] + 0.001 * grad * grad
            moment_next[at:end, :] = first
            second_next[at:end, :] = square
            master_next[at:end, :] = old - 0.001 * (
                first / (jnp.sqrt(square) + 1e-08) + 0.01 * old
            )

    halo_sent(volume, halo, halo_s, halo_r)
    halo_sent(hidden, grad_halo, gh_s, gh_r)
    for step in range(1, dps):
        peer = (dp + step) % dps
        gather_copy(dp, peer).wait_send()
        relay_copy(peer, core).wait_send()
        chip_copy(peer, dp).wait_send()
    for shard in range(dps):
        pair_copy(shard, other).wait_send()
    for step in range(1, chips):
        peer = (chip + step) % chips
        slab_copy(peer, chip).wait_send()
        total_copy(chip, peer).wait_send()
    for index in range(chips):
        total_relay(index, core).wait_send()


def per_device(volume, cotangent, master, moment, second):
    _, planes, lines, cols, width = volume.shape
    rows = master.shape[0]
    dps = lax.axis_size("dp")
    slabs = lax.axis_size("spatial")
    chips = slabs // CORES
    area = lines * cols
    block = planes * area
    half = rows // CORES
    piece = min(half, -(-half // (chips * TILE)) * TILE)
    cells_all = dps * slabs * block
    bf16, f32 = jnp.bfloat16, jnp.float32
    dma = pltpu.SemaphoreType.DMA
    vmem = pl.BlockSpec(memory_space=pltpu.VMEM)
    sizes = (dps, slabs, planes, area, cols, cells_all)
    activation, input_grad, master_next, moment_next, second_next = pl.pallas_call(
        functools.partial(layer_kernel, sizes),
        name="layer",
        out_shape=[
            jax.ShapeDtypeStruct((block, width), bf16),
            jax.ShapeDtypeStruct((block, width), bf16),
            jax.ShapeDtypeStruct((rows, width), f32),
            jax.ShapeDtypeStruct((rows, width), f32),
            jax.ShapeDtypeStruct((rows, width), f32),
        ],
        in_specs=[vmem] * 5,
        out_specs=[vmem] * 5,
        scratch_shapes=[
            pltpu.VMEM((dps * rows, width), bf16),
            pltpu.VMEM((2, area, width), bf16),
            pltpu.VMEM((2, area, width), bf16),
            pltpu.VMEM((block, width), bf16),
            pltpu.VMEM((block + 2 * area, 9 * width), bf16),
            pltpu.VMEM((9 * width, block + 2 * area), bf16),
            pltpu.VMEM((dps * rows, width), f32),
            pltpu.VMEM((dps * rows, width), bf16),
            pltpu.VMEM((dps, half, width), bf16),
            pltpu.VMEM((dps, half, width), bf16),
            pltpu.VMEM((dps, half, width), bf16),
            pltpu.VMEM((half, width), f32),
            pltpu.VMEM((half, width), bf16),
            pltpu.VMEM((chips, piece, width), bf16),
            pltpu.VMEM((CORES, chips, piece, width), bf16),
            dma((2,)),
            dma((2,)),
            dma((2,)),
            dma((2,)),
            dma((dps,)),
            dma((dps,)),
            dma((dps,)),
            dma((dps,)),
            dma((dps,)),
            dma((dps,)),
            dma((dps,)),
            dma((dps,)),
            dma((chips,)),
            dma((chips,)),
            dma((chips,)),
            dma((chips,)),
            dma((chips,)),
            dma((chips,)),
        ],
        compiler_params=pltpu.CompilerParams(
            collective_id=0, has_side_effects=True, vmem_limit_bytes=48 * 1024 * 1024
        ),
    )(
        volume.reshape(block, width),
        cotangent.reshape(block, width),
        master,
        moment,
        second,
    )
    return (
        activation.reshape(volume.shape),
        input_grad.reshape(volume.shape),
        master_next,
        moment_next,
        second_next,
    )


def solution(mesh):
    field = P("dp", "spatial", None, None, None)
    shard = P("dp", None)
    return jax.shard_map(
        per_device,
        mesh=mesh,
        in_specs=(field, field, shard, shard, shard),
        out_specs=(field, field, shard, shard, shard),
        check_vma=False,
    )
```

time: 117 us -> 42.6 us (0.36)
  blocking collectives: 48.7 us -> 0 us
  Pallas kernels: 0 us -> 33.1 us
  waiting for transfers between devices: 25.6 us -> 0 us
  matrix products: 15.3 us -> 0 us
  between operations: 14.6 us -> 0.66 us
  starting transfers between devices: 7.38 us -> 0 us
  local copies, waits for them, and re-layouts: 2.93 us -> 8.26 us
  other arithmetic: 2.34 us -> 0 us
    psum x1 -> x0, blocking collectives: 34.5 us -> none  [per_device(): shard = lax.psum(partial_grad, 'spatial')]
    pallas_call x0 -> x1, Pallas kernels: none -> 33.1 us  [per_device(): pl.pallas_call(functools.partial(layer_kernel, sizes), name='layer', out_...]
    reduce_scatter x1 -> x0, waiting for transfers between devices: 22.4 us -> none  [per_device(): lax.psum_scatter(local_grad.astype(jnp.bfloat16), 'dp', scatter_dimension...]
    dot_general x81 -> x0, matrix products: 15.3 us -> none  [the longest x27 5.53 us: weight_taps(): lax.dot_general(piece, hidden_grad, (((0,), (0,)), ((), ())), preferred_e...]
    all_gather x1 -> x0, blocking collectives: 14.2 us -> none  [per_device(): lax.all_gather(master.astype(jnp.bfloat16), 'dp', axis=0, tiled=True)]
    ppermute x4 -> x0, starting transfers between devices: 7.34 us -> none  [the longest x2 4.76 us: with_halo(): lax.ppermute(lax.slice_in_dim(block, block.shape[dim] - width, None, axis...]
    unnamed x12 -> x15, local copies, waits for them, and re-layouts: 1.62 us -> 8.26 us
    ppermute x4 -> x0, waiting for transfers between devices: 3.13 us -> none  [the longest x2 3.13 us: with_halo(): lax.ppermute(lax.slice_in_dim(block, 0, width, axis=dim), axis, backward)]
  transfers between devices with their start and end apart: 5 -> 0, of which waited for: 2 -> 0; matrix products, arithmetic and copies ran while one was open for 6% -> 0% of each run, Pallas kernels for 0% -> 0%
where the time goes in v1:
time: 42.6 us; the launch traced here: 42 us
  Pallas kernels  33.1 us (78%)
  local copies, waits for them, and re-layouts  8.26 us (19%)
  between operations  0.66 us (2%)
    pallas_call x1, Pallas kernels, per_device(): pl.pallas_call(functools.partial(layer_kernel, sizes), name='layer', out_...  33.1 us
    unnamed x15, local copies, waits for them, and re-layouts  8.26 us

profile of v1, /device:TPU:0, one launch (start us, length us, event | category | flops | bytes accessed | tf_op | source)
XLA Modules:
  0.0 42.0 jit_solution(9363704821028328309)
XLA Ops:
  0.6 0.0 copy-start
  0.6 1.0 %copy-done = f32[864,128]{1,0:T(8,128)S(1)} copy-done((f32[864,128]{1,0:T(8,128)S(1)}, f32[864,128]{1,0:T(8,128)}, u32[]{:S(2)}) %copy-start) | copy-done | bytes 442392
  1.6 0.0 copy-start.1
  1.6 1.0 %copy-done.1 = f32[864,128]{1,0:T(8,128)S(1)} copy-done((f32[864,128]{1,0:T(8,128)S(1)}, f32[864,128]{1,0:T(8,128)}, u32[]{:S(2)}) %copy-start.1) | copy-done | bytes 442392
  2.7 0.0 copy-start.2
  2.7 1.0 %copy-done.2 = f32[864,128]{1,0:T(8,128)S(1)} copy-done((f32[864,128]{1,0:T(8,128)S(1)}, f32[864,128]{1,0:T(8,128)}, u32[]{:S(2)}) %copy-start.2) | copy-done | bytes 442392
  3.7 0.0 copy-start.3
  3.7 0.8 %copy-done.3 = bf16[1,2,16,8,128]{4,3,2,1,0:T(8,128)(2,1)S(1)} copy-done((bf16[1,2,16,8,128]{4,3,2,1,0:T(8,128)(2,1)S(1)}, bf16[1,2,16,8,128]{4,3,2,1,0:T(8,128)(2,1)}, u32[]{:S(2)}) %copy-start.3) | copy-done | bytes 65560
  4.5 0.0 copy-start.4
  4.5 0.8 %copy-done.4 = bf16[1,2,16,8,128]{4,3,2,1,0:T(8,128)(2,1)S(1)} copy-done((bf16[1,2,16,8,128]{4,3,2,1,0:T(8,128)(2,1)S(1)}, bf16[1,2,16,8,128]{4,3,2,1,0:T(8,128)(2,1)}, u32[]{:S(2)}) %copy-start.4) | copy-done | bytes 65560
  5.4 33.1 %layer.1 = (bf16[256,128]{1,0:T(8,128)(2,1)S(1)}, bf16[256,128]{1,0:T(8,128)(2,1)S(1)}, f32[864,128]{1,0:T(8,128)S(1)}, f32[864,128]{1,0:T(8,128)S(1)}, f32[864,128]{1,0:T(8,128)S(1)}) custom-call(bf16[256,128]{1,0:T(8,128)(2,1)S(1)} %bitcast.4, bf16[256,128]{1,0:T(8,128)(2,1)S(1)} %bitcast.5, f32[864,128]{1,0:T(8,128)S(1)} %copy-done, ...), custom_call_target="tpu_custom_call" | custom-call | tf_op jit(solution)/shard_map/layer/pallas_call | solution.py:356
  38.4 0.6 %copy.15 = bf16[1,2,16,8,128]{4,3,2,1,0:T(8,128)(2,1)} copy(bf16[1,2,16,8,128]{4,3,2,1,0:T(8,128)(2,1)S(1)} %bitcast.7) | data formatting | bytes 131072
  39.1 0.6 %copy.16 = bf16[1,2,16,8,128]{4,3,2,1,0:T(8,128)(2,1)} copy(bf16[1,2,16,8,128]{4,3,2,1,0:T(8,128)(2,1)S(1)} %bitcast.6) | data formatting | bytes 131072
  39.7 0.8 %copy.17 = f32[864,128]{1,0:T(8,128)} copy(f32[864,128]{1,0:T(8,128)S(1)} %get-tuple-element.22) | data formatting | bytes 884736
  40.5 0.8 %copy.18 = f32[864,128]{1,0:T(8,128)} copy(f32[864,128]{1,0:T(8,128)S(1)} %get-tuple-element.23) | data formatting | bytes 884736
  41.2 0.8 %copy.19 = f32[864,128]{1,0:T(8,128)} copy(f32[864,128]{1,0:T(8,128)S(1)} %get-tuple-element.24) | data formatting | bytes 884736
Async XLA Ops:
  0.6 1.0 %copy-start = (f32[864,128]{1,0:T(8,128)S(1)}, f32[864,128]{1,0:T(8,128)}, u32[]{:S(2)}) copy-start(f32[864,128]{1,0:T(8,128)} %master.1) | copy-start | bytes 1327108
  1.6 1.0 %copy-start.1 = (f32[864,128]{1,0:T(8,128)S(1)}, f32[864,128]{1,0:T(8,128)}, u32[]{:S(2)}) copy-start(f32[864,128]{1,0:T(8,128)} %moment.1) | copy-start | bytes 1327108
  2.7 1.0 %copy-start.2 = (f32[864,128]{1,0:T(8,128)S(1)}, f32[864,128]{1,0:T(8,128)}, u32[]{:S(2)}) copy-start(f32[864,128]{1,0:T(8,128)} %second.1) | copy-start | bytes 1327108
  3.7 0.8 %copy-start.3 = (bf16[1,2,16,8,128]{4,3,2,1,0:T(8,128)(2,1)S(1)}, bf16[1,2,16,8,128]{4,3,2,1,0:T(8,128)(2,1)}, u32[]{:S(2)}) copy-start(bf16[1,2,16,8,128]{4,3,2,1,0:T(8,128)(2,1)} %param.5) | copy-start | bytes 196612
  4.5 0.8 %copy-start.4 = (bf16[1,2,16,8,128]{4,3,2,1,0:T(8,128)(2,1)S(1)}, bf16[1,2,16,8,128]{4,3,2,1,0:T(8,128)(2,1)}, u32[]{:S(2)}) copy-start(bf16[1,2,16,8,128]{4,3,2,1,0:T(8,128)(2,1)} %param.6) | copy-start | bytes 196612

commit v2 on v1

--- a/solution.py
+++ b/solution.py
@@ -10,6 +10,9 @@
 
 MESH = pl.DeviceIdType.MESH
 TILE = 16
+PARTS = 3
+VMEM_BYTES = 67043328
+SLACK = 48 * 1024
 CORES = 2
 
 
@@ -30,16 +33,21 @@
 
 def layer_kernel(
     sizes,
+    volume_hbm,
+    cotangent_hbm,
+    master_hbm,
+    moment_hbm,
+    second_hbm,
+    activation,
+    input_grad,
+    master_next,
+    moment_next,
+    second_next,
     volume,
     cotangent,
     master,
     moment,
     second,
-    activation,
-    input_grad,
-    master_next,
-    moment_next,
-    second_next,
     kernel,
     halo,
     grad_halo,
@@ -52,9 +60,10 @@
     chip_sent,
     chip_got,
     own_sum,
-    slab_sent,
-    slab_got,
+    chain_sent,
+    chain_got,
     total,
+    load_s,
     halo_s,
     halo_r,
     gh_s,
@@ -79,7 +88,7 @@
     width = volume.shape[1]
     rows = master.shape[0]
     half = rows // CORES
-    piece = total.shape[2]
+    part_rows = half // PARTS
     dp = lax.axis_index("dp")
     slab = lax.axis_index("spatial")
     core = slab % CORES
@@ -98,6 +107,21 @@
             device_id_type=MESH,
         )
 
+    loads = [
+        pltpu.make_async_copy(source, dest, load_s.at[index])
+        for index, (source, dest) in enumerate(
+            (
+                (master_hbm, master),
+                (volume_hbm, volume),
+                (cotangent_hbm, cotangent),
+                (moment_hbm, moment),
+                (second_hbm, second),
+            )
+        )
+    ]
+    for load in loads:
+        load.start()
+
     barrier = pltpu.get_barrier_semaphore()
     for step in range(1, dps):
         pl.semaphore_signal(
@@ -111,6 +135,7 @@
     def kernel_half(shard, which):
         return kernel.at[pl.ds(pl.multiple_of(shard * rows + which * half, TILE), half)]
 
+    loads[0].wait()
     kernel[pl.ds(pl.multiple_of(dp * rows, TILE), rows)] = master[...].astype(jnp.bfloat16)
     pl.semaphore_wait(barrier, dps - 1 + slabs - 1)
 
@@ -166,6 +191,7 @@
 
     for step in range(1, dps):
         gather_copy(dp, (dp + step) % dps).start()
+    loads[1].wait()
     halo_start(volume, halo, halo_s, halo_r)
 
     def put_columns(plane, at, sign, turn):
@@ -199,18 +225,22 @@
             kernel[a * group : (a + 1) * group, :],
             preferred_element_type=jnp.float32,
         )
+    loads[2].wait()
     sigma = jax.nn.sigmoid(preact)
     activation[...] = (preact * sigma).astype(jnp.bfloat16)
     slope = sigma * (1.0 + preact * (1.0 - sigma))
     hidden[...] = (cotangent[...].astype(jnp.float32) * slope).astype(jnp.bfloat16)
 
-    def pair_copy(shard, which):
-        at = pl.ds(pl.multiple_of(shard * rows + which * half, TILE), half)
+    def rows_of(k):
+        return pl.ds(k * part_rows, part_rows)
+
+    def pair_copy(shard, k, which):
+        at = pl.ds(pl.multiple_of(shard * rows + which * half + k * part_rows, TILE), part_rows)
+        flag = shard * PARTS + k
         return copy(
-            local_sent.at[at], pair_got.at[shard], pr_s.at[shard], pr_r.at[shard], (dp, pair)
-        )
-
-    next_shard = 0
+            local_sent.at[at], pair_got.at[shard, rows_of(k)], pr_s.at[flag], pr_r.at[flag], (dp, pair)
+        )
+
     for a in range(3):
         part = jnp.dot(
             turned[:, a * area : a * area + block],
@@ -219,29 +249,33 @@
         )
         local_grad[a * group : (a + 1) * group, :] = part
         local_sent[a * group : (a + 1) * group, :] = part.astype(jnp.bfloat16)
-        while next_shard < dps and (next_shard + 1) * rows <= (a + 1) * group:
-            pair_copy(next_shard, other).start()
-            next_shard += 1
         if a == 0:
             halo_start(hidden, grad_halo, gh_s, gh_r)
 
-    def own_rows(shard):
-        return local_grad[pl.ds(pl.multiple_of(shard * rows + core * half, TILE), half), :]
-
-    def chip_copy(shard, source):
+    for k in range(PARTS):
+        for step in range(dps):
+            pair_copy((dp + step) % dps, k, other).start()
+
+    def chip_rows(shard, k):
+        pair_copy(shard, k, core).wait_recv()
+        at = pl.multiple_of(shard * rows + core * half + k * part_rows, TILE)
+        return local_grad[pl.ds(at, part_rows), :] + pair_got[shard, rows_of(k)].astype(jnp.float32)
+
+    def chip_copy(shard, source, k):
         return copy(
-            chip_sent.at[shard], chip_got.at[source], ch_s.at[shard], ch_r.at[source], (shard, slab)
-        )
-
-    for step in range(1, dps):
-        shard = (dp + step) % dps
-        pair_copy(shard, core).wait_recv()
-        chip_sent[shard] = (own_rows(shard) + pair_got[shard].astype(jnp.float32)).astype(
-            jnp.bfloat16
-        )
-        chip_copy(shard, dp).start()
-    pair_copy(dp, core).wait_recv()
-    own_sum[...] = own_rows(dp) + pair_got[dp].astype(jnp.float32)
+            chip_sent.at[shard, rows_of(k)],
+            chip_got.at[source, rows_of(k)],
+            ch_s.at[shard * PARTS + k],
+            ch_r.at[source * PARTS + k],
+            (shard, slab),
+        )
+
+    for k in range(PARTS):
+        for step in range(1, dps):
+            shard = (dp + step) % dps
+            chip_sent[shard, rows_of(k)] = chip_rows(shard, k).astype(jnp.bfloat16)
+            chip_copy(shard, dp, k).start()
+        own_sum[rows_of(k)] = chip_rows(dp, k)
 
     halo_wait(hidden, grad_halo, gh_s, gh_r)
     for plane in range(planes):
@@ -260,66 +294,99 @@
             )
     input_grad[...] = back.astype(jnp.bfloat16)
 
-    for step in range(1, dps):
-        source = (dp + step) % dps
-        chip_copy(dp, source).wait_recv()
-        own_sum[...] += chip_got[source].astype(jnp.float32)
-    slab_sent[...] = own_sum[...].astype(jnp.bfloat16)
-
-    def start_of(index):
-        return jnp.minimum(index * piece, half - piece)
-
-    def slab_copy(owner, source):
-        at = pl.ds(pl.multiple_of(start_of(owner), TILE), piece)
+    low = chip < chips // 2
+    inner = jnp.where(low, chip + 1, chip - 1)
+    outer = jnp.where(low, chip - 1, chip + 1)
+    is_end = (chip == 0) | (chip == chips - 1)
+    is_middle = (chip == chips // 2 - 1) | (chip == chips // 2)
+    slot = jnp.where(is_middle, 1, 0)
+
+    def chain_copy(at, k):
+        flag = at * PARTS + k
         return copy(
-            slab_sent.at[at],
-            slab_got.at[source],
-            sl_s.at[owner],
-            sl_r.at[source],
-            (dp, owner * CORES + core),
-        )
-
-    for step in range(1, chips):
-        slab_copy((chip + step) % chips, chip).start()
-    piece_sum = own_sum[pl.ds(pl.multiple_of(start_of(chip), TILE), piece), :]
-    for step in range(1, chips):
-        source = (chip + step) % chips
-        slab_copy(chip, source).wait_recv()
-        piece_sum = piece_sum + slab_got[source].astype(jnp.float32)
-    total[core, chip] = piece_sum.astype(jnp.bfloat16)
-
-    def total_copy(source, target):
-        ref = total.at[core, source]
-        return copy(ref, ref, to_s.at[target], to_r.at[source], (dp, target * CORES + core))
-
-    def total_relay(source, which):
-        ref = total.at[which, source]
-        return copy(ref, ref, tf_s.at[source], tf_r.at[source], (dp, pair))
-
-    for step in range(1, chips):
-        total_copy(chip, (chip + step) % chips).start()
-    total_relay(chip, core).start()
-    for step in range(1, chips):
-        source = (chip + step) % chips
-        total_copy(source, chip).wait_recv()
-        total_relay(source, core).start()
-    for step in range(chips):
-        total_relay((chip + step) % chips, other).wait_recv()
+            chain_sent.at[rows_of(k)],
+            chain_got.at[at, rows_of(k)],
+            sl_s.at[k],
+            sl_r.at[flag],
+            (dp, inner * CORES + core),
+        )
+
+    def total_copy(k):
+        ref = total.at[core, rows_of(k)]
+        return copy(ref, ref, to_s.at[k], to_r.at[k], (dp, outer * CORES + core))
+
+    def total_relay(k, which):
+        ref = total.at[which, rows_of(k)]
+        return copy(ref, ref, tf_s.at[k], tf_r.at[k], (dp, pair))
+
+    def reduce_rows(k):
+        for step in range(1, dps):
+            source = (dp + step) % dps
+            chip_copy(dp, source, k).wait_recv()
+            own_sum[rows_of(k)] += chip_got[source, rows_of(k)].astype(jnp.float32)
+
+        @pl.when(is_end)
+        def _():
+            chain_sent[rows_of(k)] = own_sum[rows_of(k)].astype(jnp.bfloat16)
+            chain_copy(slot, k).start()
+
+    def pass_inward(k):
+        @pl.when(jnp.logical_not(is_end))
+        def _():
+            chain_copy(0, k).wait_recv()
+            chain_sent[rows_of(k)] = (
+                own_sum[rows_of(k)] + chain_got[0, rows_of(k)].astype(jnp.float32)
+            ).astype(jnp.bfloat16)
+            chain_copy(slot, k).start()
 
     scale = 1.0 / math.sqrt(cells_all)
-    for which in range(CORES):
-        for index in range(chips):
-            at = which * half + min(index * piece, half - piece)
-            end = at + piece
-            grad = total[which, index].astype(jnp.float32) * scale
-            old = master[at:end, :]
-            first = 0.9 * moment[at:end, :] + 0.1 * grad
-            square = 0.999 * second[at:end, :] + 0.001 * grad * grad
-            moment_next[at:end, :] = first
-            second_next[at:end, :] = square
-            master_next[at:end, :] = old - 0.001 * (
-                first / (jnp.sqrt(square) + 1e-08) + 0.01 * old
-            )
+
+    def update(k, which):
+        at = pl.ds(pl.multiple_of(which * half + k * part_rows, TILE), part_rows)
+        grad = total[which, rows_of(k)].astype(jnp.float32) * scale
+        old = master[at, :]
+        first = 0.9 * moment[at, :] + 0.1 * grad
+        square = 0.999 * second[at, :] + 0.001 * grad * grad
+        moment_next[at, :] = first
+        second_next[at, :] = square
+        master_next[at, :] = old - 0.001 * (first / (jnp.sqrt(square) + 1e-08) + 0.01 * old)
+
+    def finish(k):
+        @pl.when(is_middle)
+        def _():
+            chain_copy(1, k).wait_recv()
+            total[core, rows_of(k)] = (
+                chain_sent[rows_of(k)].astype(jnp.float32)
+                + chain_got[1, rows_of(k)].astype(jnp.float32)
+            ).astype(jnp.bfloat16)
+
+        @pl.when(jnp.logical_not(is_middle))
+        def _():
+            total_copy(k).wait_recv()
+
+        @pl.when(jnp.logical_not(is_end))
+        def _():
+            total_copy(k).start()
+
+        total_relay(k, core).start()
+        if k == 0:
+            loads[3].wait()
+            loads[4].wait()
+        update(k, core)
+
+    for k in range(PARTS):
+        reduce_rows(k)
+        if k >= 1:
+            pass_inward(k - 1)
+    finish(0)
+    pass_inward(PARTS - 1)
+    for k in range(PARTS):
+        if k >= 1:
+            finish(k)
+            total_relay(k - 1, other).wait_recv()
+            update(k - 1, other)
+    total_relay(PARTS - 1, other).wait_recv()
+    update(PARTS - 1, other)
 
     halo_sent(volume, halo, halo_s, halo_r)
     halo_sent(hidden, grad_halo, gh_s, gh_r)
@@ -327,15 +394,30 @@
         peer = (dp + step) % dps
         gather_copy(dp, peer).wait_send()
         relay_copy(peer, core).wait_send()
-        chip_copy(peer, dp).wait_send()
-    for shard in range(dps):
-        pair_copy(shard, other).wait_send()
-    for step in range(1, chips):
-        peer = (chip + step) % chips
-        slab_copy(peer, chip).wait_send()
-        total_copy(chip, peer).wait_send()
-    for index in range(chips):
-        total_relay(index, core).wait_send()
+        for k in range(PARTS):
+            chip_copy(peer, dp, k).wait_send()
+    for k in range(PARTS):
+        for shard in range(dps):
+            pair_copy(shard, k, other).wait_send()
+        chain_copy(slot, k).wait_send()
+        total_relay(k, core).wait_send()
+
+        @pl.when(jnp.logical_not(is_end))
+        def _():
+            total_copy(k).wait_send()
+
+
+def store_kernel(*refs):
+    count = (len(refs) - 1) // 2
+    flags = refs[-1]
+    stores = [
+        pltpu.make_async_copy(refs[index], refs[count + index], flags.at[index])
+        for index in range(count)
+    ]
+    for store in stores:
+        store.start()
+    for store in stores:
+        store.wait()
 
 
 def per_device(volume, cotangent, master, moment, second):
@@ -347,25 +429,33 @@
     area = lines * cols
     block = planes * area
     half = rows // CORES
-    piece = min(half, -(-half // (chips * TILE)) * TILE)
     cells_all = dps * slabs * block
     bf16, f32 = jnp.bfloat16, jnp.float32
     dma = pltpu.SemaphoreType.DMA
     vmem = pl.BlockSpec(memory_space=pltpu.VMEM)
     sizes = (dps, slabs, planes, area, cols, cells_all)
-    activation, input_grad, master_next, moment_next, second_next = pl.pallas_call(
+    out_shape = [
+        jax.ShapeDtypeStruct((block, width), bf16),
+        jax.ShapeDtypeStruct((block, width), bf16),
+        jax.ShapeDtypeStruct((rows, width), f32),
+        jax.ShapeDtypeStruct((rows, width), f32),
+        jax.ShapeDtypeStruct((rows, width), f32),
+    ]
+    held = 2 * block * width * 2 + 3 * rows * width * 4
+    grant = VMEM_BYTES - held - SLACK
+    hbm = pl.BlockSpec(memory_space=pltpu.HBM)
+    results = pl.pallas_call(
         functools.partial(layer_kernel, sizes),
         name="layer",
-        out_shape=[
-            jax.ShapeDtypeStruct((block, width), bf16),
-            jax.ShapeDtypeStruct((block, width), bf16),
-            jax.ShapeDtypeStruct((rows, width), f32),
-            jax.ShapeDtypeStruct((rows, width), f32),
-            jax.ShapeDtypeStruct((rows, width), f32),
-        ],
-        in_specs=[vmem] * 5,
+        out_shape=out_shape,
+        in_specs=[hbm] * 5,
         out_specs=[vmem] * 5,
         scratch_shapes=[
+            pltpu.VMEM((block, width), bf16),
+            pltpu.VMEM((block, width), bf16),
+            pltpu.VMEM((rows, width), f32),
+            pltpu.VMEM((rows, width), f32),
+            pltpu.VMEM((rows, width), f32),
             pltpu.VMEM((dps * rows, width), bf16),
             pltpu.VMEM((2, area, width), bf16),
             pltpu.VMEM((2, area, width), bf16),
@@ -379,8 +469,9 @@
             pltpu.VMEM((dps, half, width), bf16),
             pltpu.VMEM((half, width), f32),
             pltpu.VMEM((half, width), bf16),
-            pltpu.VMEM((chips, piece, width), bf16),
-            pltpu.VMEM((CORES, chips, piece, width), bf16),
+            pltpu.VMEM((2, half, width), bf16),
+            pltpu.VMEM((CORES, half, width), bf16),
+            dma((5,)),
             dma((2,)),
             dma((2,)),
             dma((2,)),
@@ -389,19 +480,19 @@
             dma((dps,)),
             dma((dps,)),
             dma((dps,)),
-            dma((dps,)),
-            dma((dps,)),
-            dma((dps,)),
-            dma((dps,)),
-            dma((chips,)),
-            dma((chips,)),
-            dma((chips,)),
-            dma((chips,)),
-            dma((chips,)),
-            dma((chips,)),
+            dma((dps * PARTS,)),
+            dma((dps * PARTS,)),
+            dma((dps * PARTS,)),
+            dma((dps * PARTS,)),
+            dma((PARTS,)),
+            dma((2 * PARTS,)),
+            dma((PARTS,)),
+            dma((PARTS,)),
+            dma((PARTS,)),
+            dma((PARTS,)),
         ],
         compiler_params=pltpu.CompilerParams(
-            collective_id=0, has_side_effects=True, vmem_limit_bytes=48 * 1024 * 1024
+            collective_id=0, has_side_effects=True, vmem_limit_bytes=grant
         ),
     )(
         volume.reshape(block, width),
@@ -410,6 +501,15 @@
         moment,
         second,
     )
+    activation, input_grad, master_next, moment_next, second_next = pl.pallas_call(
+        store_kernel,
+        name="store",
+        out_shape=out_shape,
+        in_specs=[vmem] * 5,
+        out_specs=[hbm] * 5,
+        scratch_shapes=[dma((5,))],
+        compiler_params=pltpu.CompilerParams(vmem_limit_bytes=grant),
+    )(*results)
     return (
         activation.reshape(volume.shape),
         input_grad.reshape(volume.shape),

time: 42.6 us -> 39.5 us (0.927); the launches traced: 42 us -> 39.3 us
  local copies, waits for them, and re-layouts: 8.26 us -> 0 us
  Pallas kernels: 33.1 us -> 38.7 us
    unnamed x15 -> x0, local copies, waits for them, and re-layouts: 8.26 us -> none
    pallas_call x1, Pallas kernels: 33.1 us -> 36.2 us  [per_device(): pl.pallas_call(functools.partial(layer_kernel, sizes), name='layer', out_...]
    pallas_call x0 -> x1, Pallas kernels: none -> 2.49 us  [per_device(): pl.pallas_call(store_kernel, name='store', out_shape=out_shape, in_specs=...]
where the time goes in v2:
time: 39.5 us; the launch traced here: 39.3 us
  Pallas kernels  38.7 us (98%)
  between operations  0.64 us (2%)
    pallas_call x1, Pallas kernels, per_device(): pl.pallas_call(functools.partial(layer_kernel, sizes), name='layer', out_...  36.2 us
    pallas_call x1, Pallas kernels, per_device(): pl.pallas_call(store_kernel, name='store', out_shape=out_shape, in_specs=...  2.49 us

profile of v2, /device:TPU:0, one launch (start us, length us, event | category | flops | bytes accessed | tf_op | source)
XLA Modules:
  0.0 39.3 jit_solution(11865357983383155345)
XLA Ops:
  0.6 36.2 %layer.1 = (bf16[256,128]{1,0:T(8,128)(2,1)}, bf16[256,128]{1,0:T(8,128)(2,1)}, f32[864,128]{1,0:T(8,128)}, f32[864,128]{1,0:T(8,128)}, f32[864,128]{1,0:T(8,128)}) custom-call(bf16[256,128]{1,0:T(8,128)(2,1)} %bitcast.4, bf16[256,128]{1,0:T(8,128)(2,1)} %bitcast.5, f32[864,128]{1,0:T(8,128)} %master_hbm.1, f32[864,128]{1,0:T(8,128)} %moment_hbm.1, ...), custom_call_target="tpu_custom_call" | custom-call | tf_op jit(solution)/shard_map/layer/pallas_call | solution.py:447
  36.8 2.5 %store.1 = (bf16[256,128]{1,0:T(8,128)(2,1)}, bf16[256,128]{1,0:T(8,128)(2,1)}, f32[864,128]{1,0:T(8,128)}, f32[864,128]{1,0:T(8,128)}, f32[864,128]{1,0:T(8,128)}) custom-call(bf16[256,128]{1,0:T(8,128)(2,1)} %get-tuple-element.15.refs_0_, bf16[256,128]{1,0:T(8,128)(2,1)} %get-tuple-element.16.refs_1_, f32[864,128]{1,0:T(8,128)} %get-tuple-element.17.refs_2_, ...), custom_call_target="tpu_custom_call" | custom-call | tf_op jit(solution)/shard_map/store/pallas_call | solution.py:504

commit v3 on v2

--- a/solution.py
+++ b/solution.py
@@ -444,10 +444,12 @@
     held = 2 * block * width * 2 + 3 * rows * width * 4
     grant = VMEM_BYTES - held - SLACK
     hbm = pl.BlockSpec(memory_space=pltpu.HBM)
+    inside = [pltpu.VMEM(leaf.shape, leaf.dtype) for leaf in out_shape]
+    outside = [pltpu.HBM(leaf.shape, leaf.dtype) for leaf in out_shape]
     results = pl.pallas_call(
         functools.partial(layer_kernel, sizes),
         name="layer",
-        out_shape=out_shape,
+        out_shape=inside,
         in_specs=[hbm] * 5,
         out_specs=[vmem] * 5,
         scratch_shapes=[
@@ -492,23 +494,28 @@
             dma((PARTS,)),
         ],
         compiler_params=pltpu.CompilerParams(
-            collective_id=0, has_side_effects=True, vmem_limit_bytes=grant
+            collective_id=0, has_side_effects=True, vmem_limit_bytes=32*1024*1024
         ),
     )(
-        volume.reshape(block, width),
-        cotangent.reshape(block, width),
-        master,
-        moment,
-        second,
+        *(
+            pltpu.with_memory_space_constraint(leaf, pltpu.HBM)
+            for leaf in (
+                volume.reshape(block, width),
+                cotangent.reshape(block, width),
+                master,
+                moment,
+                second,
+            )
+        )
     )
     activation, input_grad, master_next, moment_next, second_next = pl.pallas_call(
         store_kernel,
         name="store",
-        out_shape=out_shape,
+        out_shape=outside,
         in_specs=[vmem] * 5,
         out_specs=[hbm] * 5,
         scratch_shapes=[dma((5,))],
-        compiler_params=pltpu.CompilerParams(vmem_limit_bytes=grant),
+        compiler_params=pltpu.CompilerParams(vmem_limit_bytes=32*1024*1024),
     )(*results)
     return (
         activation.reshape(volume.shape),

time: 39.5 us -> 37 us (0.937)
  Pallas kernels: 38.7 us -> 36.2 us
    pallas_call x1, Pallas kernels: 2.49 us -> 1.14 us  [per_device(): pl.pallas_call(store_kernel, name='store', out_shape=outside, in_specs=[v...]
    pallas_call x1, Pallas kernels: 36.2 us -> 35.1 us  [per_device(): pl.pallas_call(functools.partial(layer_kernel, sizes), name='layer', out_...]
where the time goes in v3:
time: 37 us; the launch traced here: 36.8 us
  Pallas kernels  36.2 us (98%)
  between operations  0.64 us (2%)
    pallas_call x1, Pallas kernels, per_device(): pl.pallas_call(functools.partial(layer_kernel, sizes), name='layer', out_...  35.1 us
    pallas_call x1, Pallas kernels, per_device(): pl.pallas_call(store_kernel, name='store', out_shape=outside, in_specs=[v...  1.14 us

profile of v3, /device:TPU:0, one launch (start us, length us, event | category | flops | bytes accessed | tf_op | source)
XLA Modules:
  0.0 36.8 jit_solution(17506615320676668554)
XLA Ops:
  0.6 35.1 %layer.1 = (bf16[256,128]{1,0:T(8,128)(2,1)S(1)}, bf16[256,128]{1,0:T(8,128)(2,1)S(1)}, f32[864,128]{1,0:T(8,128)S(1)}, f32[864,128]{1,0:T(8,128)S(1)}, f32[864,128]{1,0:T(8,128)S(1)}) custom-call(bf16[256,128]{1,0:T(8,128)(2,1)} %bitcast.4, bf16[256,128]{1,0:T(8,128)(2,1)} %bitcast.5, f32[864,128]{1,0:T(8,128)} %master_hbm.1, f32[864,128]{1,0:T(8,128)} %moment_hbm.1, ...), custom_call_target="tpu_custom_call" | custom-call | tf_op jit(solution)/shard_map/layer/pallas_call | solution.py:449
  35.7 1.1 %store.1 = (bf16[256,128]{1,0:T(8,128)(2,1)}, bf16[256,128]{1,0:T(8,128)(2,1)}, f32[864,128]{1,0:T(8,128)}, f32[864,128]{1,0:T(8,128)}, f32[864,128]{1,0:T(8,128)}) custom-call(bf16[256,128]{1,0:T(8,128)(2,1)S(1)} %get-tuple-element.15.refs_0_, bf16[256,128]{1,0:T(8,128)(2,1)S(1)} %get-tuple-element.16.refs_1_, f32[864,128]{1,0:T(8,128)S(1)} %get-tuple-element.17.refs_2_, ...), custom_call_target="tpu_custom_call" | custom-call | tf_op jit(solution)/shard_map/store/pallas_call | solution.py:511

commit v4 on v3

--- a/solution.py
+++ b/solution.py
@@ -10,7 +10,8 @@
 
 MESH = pl.DeviceIdType.MESH
 TILE = 16
-PARTS = 3
+PARTS = 9
+LAG = 4
 VMEM_BYTES = 67043328
 SLACK = 48 * 1024
 CORES = 2
@@ -127,17 +128,27 @@
         pl.semaphore_signal(
             barrier, inc=1, device_id=((dp + step) % dps, slab), device_id_type=MESH
         )
-    for step in range(1, slabs):
-        pl.semaphore_signal(
-            barrier, inc=1, device_id=(dp, (slab + step) % slabs), device_id_type=MESH
-        )
-
-    def kernel_half(shard, which):
-        return kernel.at[pl.ds(pl.multiple_of(shard * rows + which * half, TILE), half)]
+    for gap in (1, 2):
+
+        @pl.when(slab + gap < slabs)
+        def _():
+            pl.semaphore_signal(barrier, inc=1, device_id=(dp, slab + gap), device_id_type=MESH)
+
+        @pl.when(slab >= gap)
+        def _():
+            pl.semaphore_signal(barrier, inc=1, device_id=(dp, slab - gap), device_id_type=MESH)
+
+    beside = jnp.minimum(slab, 2) + jnp.minimum(slabs - 1 - slab, 2)
+    cut = half // (2 * TILE) * TILE
+    spans = ((0, cut), (cut, half - cut))
+
+    def kernel_span(shard, which, p):
+        at = pl.multiple_of(shard * rows + which * half + spans[p][0], TILE)
+        return kernel.at[pl.ds(at, spans[p][1])]
 
     loads[0].wait()
     kernel[pl.ds(pl.multiple_of(dp * rows, TILE), rows)] = master[...].astype(jnp.bfloat16)
-    pl.semaphore_wait(barrier, dps - 1 + slabs - 1)
+    pl.semaphore_wait(barrier, dps - 1 + beside)
 
     def halo_copy(source, dest, send, recv, side):
         if side == 0:
@@ -181,16 +192,33 @@
         def _():
             dest[1] = jnp.zeros((area, width), jnp.bfloat16)
 
-    def gather_copy(shard, target):
-        mine = kernel_half(shard, core)
-        return copy(mine, mine, ag_s.at[target], ag_r.at[shard], (target, slab))
-
-    def relay_copy(shard, which):
-        mine = kernel_half(shard, which)
-        return copy(mine, mine, fw_s.at[shard], fw_r.at[shard], (dp, pair))
-
-    for step in range(1, dps):
-        gather_copy(dp, (dp + step) % dps).start()
+    def gather_copy(shard, target, p, lane):
+        ref = kernel_span(shard, core, p)
+        return copy(ref, ref, ag_s.at[lane * 2 + p], ag_r.at[shard * 2 + p], (target, slab))
+
+    def relay_copy(shard, p, which):
+        ref = kernel_span(shard, which, p)
+        return copy(ref, ref, fw_s.at[shard * 2 + p], fw_r.at[shard * 2 + p], (dp, pair))
+
+    def relay(shard, p):
+        gather_copy(shard, dp, p, shard).wait_recv()
+        relay_copy(shard, p, core).start()
+
+    square_grid = dps == 4
+    peers = [(dp + step) % dps for step in range(1, dps)]
+    sends = [(dp, peer, p, peer) for peer in peers for p in (0, 1)]
+    early, late = [], [(peer, p) for peer in peers for p in (0, 1)]
+    if square_grid:
+        near = dp + 1 - 2 * (dp % 2)
+        far = dp + 2 - 4 * (dp // 2)
+        across = dps - 1 - dp
+        peers = [near, far, across]
+        sends = [(dp, near, 0, near), (dp, far, 1, far), (dp, near, 1, near), (dp, far, 0, far)]
+        passes = [(near, far, 0, across), (far, near, 1, across)]
+        early = [(near, 0), (far, 1)]
+        late = [(near, 1), (far, 0), (across, 0), (across, 1)]
+    for send in sends:
+        gather_copy(*send).start()
     loads[1].wait()
     halo_start(volume, halo, halo_s, halo_r)
 
@@ -206,16 +234,18 @@
 
     for plane in range(planes):
         put_columns(volume[plane * area : (plane + 1) * area], plane + 1, 1, True)
+    for index, (shard, p) in enumerate(early):
+        gather_copy(shard, dp, p, shard).wait_recv()
+        gather_copy(*passes[index]).start()
+        relay_copy(shard, p, core).start()
     halo_wait(volume, halo, halo_s, halo_r)
     put_columns(halo[0], 0, 1, True)
     put_columns(halo[1], planes + 1, 1, True)
 
-    for step in range(1, dps):
-        source = (dp + step) % dps
-        gather_copy(source, dp).wait_recv()
-        relay_copy(source, core).start()
-    for step in range(1, dps):
-        relay_copy((dp + step) % dps, other).wait_recv()
+    for shard, p in late:
+        relay(shard, p)
+    for shard, p in early + late:
+        relay_copy(shard, p, other).wait_recv()
 
     group = 9 * width
     preact = jnp.zeros((block, width), jnp.float32)
@@ -374,26 +404,30 @@
             loads[4].wait()
         update(k, core)
 
-    for k in range(PARTS):
-        reduce_rows(k)
-        if k >= 1:
-            pass_inward(k - 1)
-    finish(0)
-    pass_inward(PARTS - 1)
-    for k in range(PARTS):
-        if k >= 1:
-            finish(k)
-            total_relay(k - 1, other).wait_recv()
-            update(k - 1, other)
-    total_relay(PARTS - 1, other).wait_recv()
-    update(PARTS - 1, other)
+    def finish_other(k):
+        total_relay(k, other).wait_recv()
+        update(k, other)
+
+    for step in range(PARTS + 2 * LAG):
+        if step < PARTS:
+            reduce_rows(step)
+        if 0 <= step - LAG < PARTS:
+            pass_inward(step - LAG)
+        if 0 <= step - 2 * LAG < PARTS:
+            finish(step - 2 * LAG)
+        if 0 <= step - 2 * LAG - 2 < PARTS:
+            finish_other(step - 2 * LAG - 2)
+    for k in range(PARTS - 2, PARTS):
+        finish_other(k)
 
     halo_sent(volume, halo, halo_s, halo_r)
     halo_sent(hidden, grad_halo, gh_s, gh_r)
+    for send in sends + (passes if square_grid else []):
+        gather_copy(*send).wait_send()
+    for shard, p in early + late:
+        relay_copy(shard, p, core).wait_send()
     for step in range(1, dps):
         peer = (dp + step) % dps
-        gather_copy(dp, peer).wait_send()
-        relay_copy(peer, core).wait_send()
         for k in range(PARTS):
             chip_copy(peer, dp, k).wait_send()
     for k in range(PARTS):
@@ -478,10 +512,10 @@
             dma((2,)),
             dma((2,)),
             dma((2,)),
-            dma((dps,)),
-            dma((dps,)),
-            dma((dps,)),
-            dma((dps,)),
+            dma((2 * dps,)),
+            dma((2 * dps,)),
+            dma((2 * dps,)),
+            dma((2 * dps,)),
             dma((dps * PARTS,)),
             dma((dps * PARTS,)),
             dma((dps * PARTS,)),

time: 37 us -> 35.9 us (0.970)
  Pallas kernels: 36.2 us -> 35.1 us
    pallas_call x1, Pallas kernels: 35.1 us -> 33.9 us  [per_device(): pl.pallas_call(functools.partial(layer_kernel, sizes), name='layer', out_...]
where the time goes in v4:
time: 35.9 us; the launch traced here: 35.7 us
  Pallas kernels  35.1 us (98%)
  between operations  0.64 us (2%)
    pallas_call x1, Pallas kernels, per_device(): pl.pallas_call(functools.partial(layer_kernel, sizes), name='layer', out_...  33.9 us
    pallas_call x1, Pallas kernels, per_device(): pl.pallas_call(store_kernel, name='store', out_shape=outside, in_specs=[v...  1.14 us

profile of v4, /device:TPU:0, one launch (start us, length us, event | category | flops | bytes accessed | tf_op | source)
XLA Modules:
  0.0 35.7 jit_solution(17916490029369905182)
XLA Ops:
  0.6 33.9 %layer.1 = (bf16[256,128]{1,0:T(8,128)(2,1)S(1)}, bf16[256,128]{1,0:T(8,128)(2,1)S(1)}, f32[864,128]{1,0:T(8,128)S(1)}, f32[864,128]{1,0:T(8,128)S(1)}, f32[864,128]{1,0:T(8,128)S(1)}) custom-call(bf16[256,128]{1,0:T(8,128)(2,1)} %bitcast.4, bf16[256,128]{1,0:T(8,128)(2,1)} %bitcast.5, f32[864,128]{1,0:T(8,128)} %master_hbm.1, f32[864,128]{1,0:T(8,128)} %moment_hbm.1, ...), custom_call_target="tpu_custom_call" | custom-call | tf_op jit(solution)/shard_map/layer/pallas_call | solution.py:483
  34.6 1.1 %store.1 = (bf16[256,128]{1,0:T(8,128)(2,1)}, bf16[256,128]{1,0:T(8,128)(2,1)}, f32[864,128]{1,0:T(8,128)}, f32[864,128]{1,0:T(8,128)}, f32[864,128]{1,0:T(8,128)}) custom-call(bf16[256,128]{1,0:T(8,128)(2,1)S(1)} %get-tuple-element.15.refs_0_, bf16[256,128]{1,0:T(8,128)(2,1)S(1)} %get-tuple-element.16.refs_1_, f32[864,128]{1,0:T(8,128)S(1)} %get-tuple-element.17.refs_2_, ...), custom_call_target="tpu_custom_call" | custom-call | tf_op jit(solution)/shard_map/store/pallas_call | solution.py:545

commit v5 on v4

--- a/solution.py
+++ b/solution.py
@@ -61,8 +61,8 @@
     chip_sent,
     chip_got,
     own_sum,
-    chain_sent,
-    chain_got,
+    hop_sent,
+    hop_got,
     total,
     load_s,
     halo_s,
@@ -79,8 +79,6 @@
     ch_r,
     sl_s,
     sl_r,
-    to_s,
-    to_r,
     tf_s,
     tf_r,
 ):
@@ -128,17 +126,19 @@
         pl.semaphore_signal(
             barrier, inc=1, device_id=((dp + step) % dps, slab), device_id_type=MESH
         )
-    for gap in (1, 2):
-
-        @pl.when(slab + gap < slabs)
-        def _():
-            pl.semaphore_signal(barrier, inc=1, device_id=(dp, slab + gap), device_id_type=MESH)
-
-        @pl.when(slab >= gap)
-        def _():
-            pl.semaphore_signal(barrier, inc=1, device_id=(dp, slab - gap), device_id_type=MESH)
-
-    beside = jnp.minimum(slab, 2) + jnp.minimum(slabs - 1 - slab, 2)
+    @pl.when(slab + 1 < slabs)
+    def _():
+        pl.semaphore_signal(barrier, inc=1, device_id=(dp, slab + 1), device_id_type=MESH)
+
+    @pl.when(slab >= 1)
+    def _():
+        pl.semaphore_signal(barrier, inc=1, device_id=(dp, slab - 1), device_id_type=MESH)
+
+    hops = chips.bit_length() - 1
+    partners = [(chip + gap * (1 - 2 * (chip // gap % 2))) * CORES + core for gap in [2**h for h in range(hops)]]
+    for partner in partners:
+        pl.semaphore_signal(barrier, inc=1, device_id=(dp, partner), device_id_type=MESH)
+    beside = jnp.minimum(slab, 1) + jnp.minimum(slabs - 1 - slab, 1) + hops
     cut = half // (2 * TILE) * TILE
     spans = ((0, cut), (cut, half - cut))
 
@@ -324,26 +324,15 @@
             )
     input_grad[...] = back.astype(jnp.bfloat16)
 
-    low = chip < chips // 2
-    inner = jnp.where(low, chip + 1, chip - 1)
-    outer = jnp.where(low, chip - 1, chip + 1)
-    is_end = (chip == 0) | (chip == chips - 1)
-    is_middle = (chip == chips // 2 - 1) | (chip == chips // 2)
-    slot = jnp.where(is_middle, 1, 0)
-
-    def chain_copy(at, k):
-        flag = at * PARTS + k
+    def hop_copy(h, k):
+        flag = h * PARTS + k
         return copy(
-            chain_sent.at[rows_of(k)],
-            chain_got.at[at, rows_of(k)],
-            sl_s.at[k],
+            hop_sent.at[h, rows_of(k)],
+            hop_got.at[h, rows_of(k)],
+            sl_s.at[flag],
             sl_r.at[flag],
-            (dp, inner * CORES + core),
-        )
-
-    def total_copy(k):
-        ref = total.at[core, rows_of(k)]
-        return copy(ref, ref, to_s.at[k], to_r.at[k], (dp, outer * CORES + core))
+            (dp, partners[h]),
+        )
 
     def total_relay(k, which):
         ref = total.at[which, rows_of(k)]
@@ -355,19 +344,17 @@
             chip_copy(dp, source, k).wait_recv()
             own_sum[rows_of(k)] += chip_got[source, rows_of(k)].astype(jnp.float32)
 
-        @pl.when(is_end)
-        def _():
-            chain_sent[rows_of(k)] = own_sum[rows_of(k)].astype(jnp.bfloat16)
-            chain_copy(slot, k).start()
-
-    def pass_inward(k):
-        @pl.when(jnp.logical_not(is_end))
-        def _():
-            chain_copy(0, k).wait_recv()
-            chain_sent[rows_of(k)] = (
-                own_sum[rows_of(k)] + chain_got[0, rows_of(k)].astype(jnp.float32)
-            ).astype(jnp.bfloat16)
-            chain_copy(slot, k).start()
+        hop_sent[0, rows_of(k)] = own_sum[rows_of(k)].astype(jnp.bfloat16)
+        hop_copy(0, k).start()
+
+    def hop_sum(h, k):
+        hop_copy(h, k).wait_recv()
+        mine = hop_sent[h, rows_of(k)].astype(jnp.float32)
+        return (mine + hop_got[h, rows_of(k)].astype(jnp.float32)).astype(jnp.bfloat16)
+
+    def pass_on(h, k):
+        hop_sent[h, rows_of(k)] = hop_sum(h - 1, k)
+        hop_copy(h, k).start()
 
     scale = 1.0 / math.sqrt(cells_all)
 
@@ -382,22 +369,7 @@
         master_next[at, :] = old - 0.001 * (first / (jnp.sqrt(square) + 1e-08) + 0.01 * old)
 
     def finish(k):
-        @pl.when(is_middle)
-        def _():
-            chain_copy(1, k).wait_recv()
-            total[core, rows_of(k)] = (
-                chain_sent[rows_of(k)].astype(jnp.float32)
-                + chain_got[1, rows_of(k)].astype(jnp.float32)
-            ).astype(jnp.bfloat16)
-
-        @pl.when(jnp.logical_not(is_middle))
-        def _():
-            total_copy(k).wait_recv()
-
-        @pl.when(jnp.logical_not(is_end))
-        def _():
-            total_copy(k).start()
-
+        total[core, rows_of(k)] = hop_sum(hops - 1, k)
         total_relay(k, core).start()
         if k == 0:
             loads[3].wait()
@@ -408,15 +380,17 @@
         total_relay(k, other).wait_recv()
         update(k, other)
 
-    for step in range(PARTS + 2 * LAG):
+    last = hops * LAG
+    for step in range(PARTS + last):
         if step < PARTS:
             reduce_rows(step)
-        if 0 <= step - LAG < PARTS:
-            pass_inward(step - LAG)
-        if 0 <= step - 2 * LAG < PARTS:
-            finish(step - 2 * LAG)
-        if 0 <= step - 2 * LAG - 2 < PARTS:
-            finish_other(step - 2 * LAG - 2)
+        for h in range(1, hops):
+            if 0 <= step - h * LAG < PARTS:
+                pass_on(h, step - h * LAG)
+        if 0 <= step - last < PARTS:
+            finish(step - last)
+        if 0 <= step - last - 2 < PARTS:
+            finish_other(step - last - 2)
     for k in range(PARTS - 2, PARTS):
         finish_other(k)
 
@@ -433,12 +407,9 @@
     for k in range(PARTS):
         for shard in range(dps):
             pair_copy(shard, k, other).wait_send()
-        chain_copy(slot, k).wait_send()
+        for h in range(hops):
+            hop_copy(h, k).wait_send()
         total_relay(k, core).wait_send()
-
-        @pl.when(jnp.logical_not(is_end))
-        def _():
-            total_copy(k).wait_send()
 
 
 def store_kernel(*refs):
@@ -460,6 +431,7 @@
     dps = lax.axis_size("dp")
     slabs = lax.axis_size("spatial")
     chips = slabs // CORES
+    hops = chips.bit_length() - 1
     area = lines * cols
     block = planes * area
     half = rows // CORES
@@ -504,8 +476,8 @@
             pltpu.VMEM((dps, half, width), bf16),
             pltpu.VMEM((dps, half, width), bf16),
             pltpu.VMEM((half, width), f32),
-            pltpu.VMEM((half, width), bf16),
-            pltpu.VMEM((2, half, width), bf16),
+            pltpu.VMEM((hops, half, width), bf16),
+            pltpu.VMEM((hops, half, width), bf16),
             pltpu.VMEM((CORES, half, width), bf16),
             dma((5,)),
             dma((2,)),
@@ -520,10 +492,8 @@
             dma((dps * PARTS,)),
             dma((dps * PARTS,)),
             dma((dps * PARTS,)),
-            dma((PARTS,)),
-            dma((2 * PARTS,)),
-            dma((PARTS,)),
-            dma((PARTS,)),
+            dma((hops * PARTS,)),
+            dma((hops * PARTS,)),
             dma((PARTS,)),
             dma((PARTS,)),
         ],

time: 35.9 us -> 35.1 us (0.978)
  Pallas kernels: 35.1 us -> 34.3 us
    pallas_call x1, Pallas kernels: 33.9 us -> 33.1 us  [per_device(): pl.pallas_call(functools.partial(layer_kernel, sizes), name='layer', out_...]
where the time goes in v5:
time: 35.1 us; the launch traced here: 34.9 us
  Pallas kernels  34.3 us (98%)
  between operations  0.64 us (2%)
    pallas_call x1, Pallas kernels, per_device(): pl.pallas_call(functools.partial(layer_kernel, sizes), name='layer', out_...  33.1 us
    pallas_call x1, Pallas kernels, per_device(): pl.pallas_call(store_kernel, name='store', out_shape=outside, in_specs=[v...  1.14 us

profile of v5, /device:TPU:0, one launch (start us, length us, event | category | flops | bytes accessed | tf_op | source)
XLA Modules:
  0.0 34.9 jit_solution(8103826644439937001)
XLA Ops:
  0.6 33.1 %layer.1 = (bf16[256,128]{1,0:T(8,128)(2,1)S(1)}, bf16[256,128]{1,0:T(8,128)(2,1)S(1)}, f32[864,128]{1,0:T(8,128)S(1)}, f32[864,128]{1,0:T(8,128)S(1)}, f32[864,128]{1,0:T(8,128)S(1)}) custom-call(bf16[256,128]{1,0:T(8,128)(2,1)} %bitcast.4, bf16[256,128]{1,0:T(8,128)(2,1)} %bitcast.5, f32[864,128]{1,0:T(8,128)} %master_hbm.1, f32[864,128]{1,0:T(8,128)} %moment_hbm.1, ...), custom_call_target="tpu_custom_call" | custom-call | tf_op jit(solution)/shard_map/layer/pallas_call | solution.py:455
  33.8 1.1 %store.1 = (bf16[256,128]{1,0:T(8,128)(2,1)}, bf16[256,128]{1,0:T(8,128)(2,1)}, f32[864,128]{1,0:T(8,128)}, f32[864,128]{1,0:T(8,128)}, f32[864,128]{1,0:T(8,128)}) custom-call(bf16[256,128]{1,0:T(8,128)(2,1)S(1)} %get-tuple-element.15.refs_0_, bf16[256,128]{1,0:T(8,128)(2,1)S(1)} %get-tuple-element.16.refs_1_, f32[864,128]{1,0:T(8,128)S(1)} %get-tuple-element.17.refs_2_, ...), custom_call_target="tpu_custom_call" | custom-call | tf_op jit(solution)/shard_map/store/pallas_call | solution.py:515

commit v6 on v5

--- a/solution.py
+++ b/solution.py
@@ -10,8 +10,8 @@
 
 MESH = pl.DeviceIdType.MESH
 TILE = 16
-PARTS = 9
-LAG = 4
+PARTS = 3
+LAG = 2
 VMEM_BYTES = 67043328
 SLACK = 48 * 1024
 CORES = 2

time: 35.1 us -> 32.5 us (0.926)
  Pallas kernels: 34.3 us -> 31.7 us
    pallas_call x1, Pallas kernels: 33.1 us -> 30.5 us  [per_device(): pl.pallas_call(functools.partial(layer_kernel, sizes), name='layer', out_...]
where the time goes in v6:
time: 32.5 us; the launch traced here: 32.3 us
  Pallas kernels  31.7 us (98%)
  between operations  0.64 us (2%)
    pallas_call x1, Pallas kernels, per_device(): pl.pallas_call(functools.partial(layer_kernel, sizes), name='layer', out_...  30.5 us
    pallas_call x1, Pallas kernels, per_device(): pl.pallas_call(store_kernel, name='store', out_shape=outside, in_specs=[v...  1.14 us

profile of v6, /device:TPU:0, one launch (start us, length us, event | category | flops | bytes accessed | tf_op | source)
XLA Modules:
  0.0 32.3 jit_solution(10264817541470753819)
XLA Ops:
  0.6 30.5 %layer.1 = (bf16[256,128]{1,0:T(8,128)(2,1)S(1)}, bf16[256,128]{1,0:T(8,128)(2,1)S(1)}, f32[864,128]{1,0:T(8,128)S(1)}, f32[864,128]{1,0:T(8,128)S(1)}, f32[864,128]{1,0:T(8,128)S(1)}) custom-call(bf16[256,128]{1,0:T(8,128)(2,1)} %bitcast.4, bf16[256,128]{1,0:T(8,128)(2,1)} %bitcast.5, f32[864,128]{1,0:T(8,128)} %master_hbm.1, f32[864,128]{1,0:T(8,128)} %moment_hbm.1, ...), custom_call_target="tpu_custom_call" | custom-call | tf_op jit(solution)/shard_map/layer/pallas_call | solution.py:455
  31.2 1.1 %store.1 = (bf16[256,128]{1,0:T(8,128)(2,1)}, bf16[256,128]{1,0:T(8,128)(2,1)}, f32[864,128]{1,0:T(8,128)}, f32[864,128]{1,0:T(8,128)}, f32[864,128]{1,0:T(8,128)}) custom-call(bf16[256,128]{1,0:T(8,128)(2,1)S(1)} %get-tuple-element.15.refs_0_, bf16[256,128]{1,0:T(8,128)(2,1)S(1)} %get-tuple-element.16.refs_1_, f32[864,128]{1,0:T(8,128)S(1)} %get-tuple-element.17.refs_2_, ...), custom_call_target="tpu_custom_call" | custom-call | tf_op jit(solution)/shard_map/store/pallas_call | solution.py:515

commit v7 on v6

--- a/solution.py
+++ b/solution.py
@@ -11,7 +11,7 @@
 MESH = pl.DeviceIdType.MESH
 TILE = 16
 PARTS = 3
-LAG = 2
+LAG = 3
 VMEM_BYTES = 67043328
 SLACK = 48 * 1024
 CORES = 2

time: 32.5 us -> 32.5 us (level)
  no operation moved by 1% of the time
where the time goes in v7:
time: 32.5 us; the launch traced here: 32.3 us
  Pallas kernels  31.7 us (98%)
  between operations  0.64 us (2%)
    pallas_call x1, Pallas kernels, per_device(): pl.pallas_call(functools.partial(layer_kernel, sizes), name='layer', out_...  30.5 us
    pallas_call x1, Pallas kernels, per_device(): pl.pallas_call(store_kernel, name='store', out_shape=outside, in_specs=[v...  1.14 us

profile of v7, /device:TPU:0, one launch (start us, length us, event | category | flops | bytes accessed | tf_op | source)
XLA Modules:
  0.0 32.3 jit_solution(10264817541470753819)
XLA Ops:
  0.6 30.5 %layer.1 = (bf16[256,128]{1,0:T(8,128)(2,1)S(1)}, bf16[256,128]{1,0:T(8,128)(2,1)S(1)}, f32[864,128]{1,0:T(8,128)S(1)}, f32[864,128]{1,0:T(8,128)S(1)}, f32[864,128]{1,0:T(8,128)S(1)}) custom-call(bf16[256,128]{1,0:T(8,128)(2,1)} %bitcast.4, bf16[256,128]{1,0:T(8,128)(2,1)} %bitcast.5, f32[864,128]{1,0:T(8,128)} %master_hbm.1, f32[864,128]{1,0:T(8,128)} %moment_hbm.1, ...), custom_call_target="tpu_custom_call" | custom-call | tf_op jit(solution)/shard_map/layer/pallas_call | solution.py:455
  31.2 1.1 %store.1 = (bf16[256,128]{1,0:T(8,128)(2,1)}, bf16[256,128]{1,0:T(8,128)(2,1)}, f32[864,128]{1,0:T(8,128)}, f32[864,128]{1,0:T(8,128)}, f32[864,128]{1,0:T(8,128)}) custom-call(bf16[256,128]{1,0:T(8,128)(2,1)S(1)} %get-tuple-element.15.refs_0_, bf16[256,128]{1,0:T(8,128)(2,1)S(1)} %get-tuple-element.16.refs_1_, f32[864,128]{1,0:T(8,128)S(1)} %get-tuple-element.17.refs_2_, ...), custom_call_target="tpu_custom_call" | custom-call | tf_op jit(solution)/shard_map/store/pallas_call | solution.py:515
